TPU v7x, 32 devices: a whole 2x2x4 slice. The times are simulated.
32 devices in a mesh: group: 4 (over x, core), prompt: 8 (over z, y).
Axes of the slice: x: 2, y: 2, z: 4, core: 2. Of those that a mesh axis runs over, the one named last changes fastest.
Arguments:
- queries: bfloat16 [8, 4, 64, 3072], P('prompt', 'group'), may hold values from -48 to 48
- fresh_latent: bfloat16 [8, 4, 64, 576], P('prompt', 'group'), may hold values from -6 to 6
- latent_cache: bfloat16 [8, 4, 512, 576], P('prompt', 'group'), may hold values from -48 to 48
- selected: int32 [8, 4, 64], P('prompt', 'group'), may hold values from 0 to 511, as said below
- position: int32 [8, 4], P('prompt'), may hold values from 0 to 3, each once within a row
- latent_gain: bfloat16 [512], replicated, may hold values from 0.099609375 to 1.8984375
- kv_up: bfloat16 [512, 4096], P('prompt'), may hold values from -0.25 to 0.25
- out_weight: bfloat16 [2048, 2048], P('prompt'), may hold values from -0.125 to 0.125
Outputs:
- attended: bfloat16 [8, 4, 64, 2048], P('prompt', 'group')
- blended: bfloat16 [8, 4, 512, 576], P('prompt', 'group')
Inputs may be any that keep to these rules, and one draw needn't show every extreme that they name: `selected`: the 64 indices of a group are distinct and increasing.
All inputs are finite; a program needn't handle non-finite values.
Results may differ from a plain program's by a relative error of at most 0.011.
Values may be sent and summed in bfloat16 or wider, within the bound.
No kernel may reach another device: no remote copies, remote signals or barrier semaphores. Data moves between devices by JAX's collectives and lax.ppermute only.
A program may use at most 128 MiB of HBM per device.

v0:
```python
import jax
import jax.numpy as jnp
from jax import lax
from jax.sharding import PartitionSpec as P

D = 2048
H = 16
DN = 128
DR = 64
DV = 128
LAT = 512


def rope_rotate(values, places):
    half = values.shape[-1] // 2
    freqs = 10000.0 ** (-jnp.arange(half, dtype=jnp.float32) / half)
    angles = places[..., None] * freqs
    cosine = jnp.cos(angles)
    sine = jnp.sin(angles)
    first = values[..., :half]
    second = values[..., half:]
    return jnp.concatenate([first * cosine - second * sine, second * cosine + first * sine], -1)


def prepare_rows(fresh, gain, places):
    latent = fresh[..., :LAT].astype(jnp.float32)
    factor = lax.rsqrt(jnp.mean(latent * latent, -1, keepdims=True) + 1e-06)
    normed = latent * factor * gain.astype(jnp.float32)
    turned = rope_rotate(fresh[..., LAT:].astype(jnp.float32), places)
    return jnp.concatenate([normed, turned], -1).astype(jnp.bfloat16)


def shards(queries, fresh_latent, latent_cache, selected, position, latent_gain, kv_up, out_weight):
    prompts, groups, picks, _ = queries.shape
    length = latent_cache.shape[2]
    first_group = lax.axis_index("group") * groups
    own_order = lax.dynamic_slice_in_dim(position, first_group, groups, 1)
    place_int = own_order[:, :, None] * length + selected
    places = place_int.astype(jnp.float32)
    fresh_rows = prepare_rows(fresh_latent, latent_gain, places)
    prompt_ids = jnp.arange(prompts, dtype=jnp.int32)[:, None, None]
    group_ids = jnp.arange(groups, dtype=jnp.int32)[None, :, None]
    blended = latent_cache.at[prompt_ids, group_ids, selected].set(fresh_rows)
    whole_kv = lax.all_gather(kv_up, "prompt", axis=0, tiled=True).reshape(LAT, H, DN + DV)
    shaped = queries.reshape(prompts, groups, picks, H, DN + DR)
    absorbed = jnp.einsum(
        "pcshd,lhd->pcshl", shaped[..., :DN], whole_kv[..., :DN], preferred_element_type=jnp.float32
    ).astype(jnp.bfloat16)
    turned = rope_rotate(shaped[..., DN:].astype(jnp.float32), places[..., None]).astype(
        jnp.bfloat16
    )
    rows = groups * picks
    query_vec = jnp.concatenate([absorbed, turned], -1).reshape(prompts, rows, H, LAT + DR)
    query_place = place_int.reshape(prompts, rows)
    scale = (DN + DR) ** (-0.5)
    offsets = jnp.arange(length, dtype=jnp.int32)

    def update(state, keys, key_place):
        peak, total, mixed = state
        allowed = (key_place[:, None, :] <= query_place[:, :, None])[:, :, None, :]
        scores = (
            jnp.einsum("pqhe,pke->pqhk", query_vec, keys, preferred_element_type=jnp.float32)
            * scale
        )
        block_peak = jnp.max(jnp.where(allowed, scores, -1e30), -1)
        new_peak = jnp.maximum(peak, block_peak)
        probs = jnp.where(allowed, jnp.exp(scores - new_peak[..., None]), 0.0)
        decay = jnp.exp(peak - new_peak)
        total = total * decay + jnp.sum(probs, -1)
        mixed = mixed * decay[..., None] + jnp.einsum(
            "pqhk,pkl->pqhl",
            probs.astype(jnp.bfloat16),
            keys[..., :LAT],
            preferred_element_type=jnp.float32,
        )
        return (new_peak, total, mixed)

    start_state = (
        jnp.full((prompts, rows, H), -1e30, jnp.float32),
        jnp.zeros((prompts, rows, H), jnp.float32),
        jnp.zeros((prompts, rows, H, LAT), jnp.float32),
    )
    piece = lax.all_gather(blended, "group", axis=1, tiled=True)

    def one_group(index, carry):
        keys = lax.dynamic_slice_in_dim(piece, index, 1, 1)[:, 0]
        order = lax.dynamic_slice_in_dim(position, index, 1, 1)
        key_place = order * length + offsets[None, :]
        needed = jnp.any(key_place[:, :1] <= jnp.max(query_place, -1, keepdims=True))
        return lax.cond(needed, lambda c: update(c, keys, key_place), lambda c: c, carry)

    peak, total, mixed = lax.fori_loop(0, piece.shape[1], one_group, start_state)
    latent_mix = (mixed / total[..., None]).astype(jnp.bfloat16)
    heads = jnp.einsum(
        "pqhl,lhv->pqhv", latent_mix, whole_kv[..., DN:], preferred_element_type=jnp.float32
    ).astype(jnp.bfloat16)
    heads = heads.reshape(prompts * rows, H * DV)
    whole_out = lax.all_gather(out_weight, "prompt", axis=0, tiled=True)
    attended = jnp.dot(heads, whole_out, preferred_element_type=jnp.float32)
    return (attended.astype(jnp.bfloat16).reshape(prompts, groups, picks, D), blended)


def solution(mesh):
    in_specs = (
        P("prompt", "group", None, None),
        P("prompt", "group", None, None),
        P("prompt", "group", None, None),
        P("prompt", "group", None),
        P("prompt", None),
        P(),
        P("prompt", None),
        P("prompt", None),
    )
    out_specs = (P("prompt", "group", None, None), P("prompt", "group", None, None))
    return jax.shard_map(shards, mesh=mesh, in_specs=in_specs, out_specs=out_specs, check_vma=False)
```

profile of v0, /device:TPU:0, one launch (start us, length us, event | category | flops | bytes accessed | tf_op | source)
XLA Modules:
  0.0 257.9 jit_solution(10808461061996770025)
XLA Ops:
  7.2 0.8 slice.44
  8.0 1.0 fusion.33
  9.0 1.2 fusion.52
  10.3 1.3 convert_bitcast_fusion
  12.0 1.4 copy.49
  13.4 0.7 convert_element_type.80
  14.1 0.9 fusion.35
  15.0 1.3 scatter_custom_fusion
  16.4 0.8 copy-done.1
  17.3 0.7 all-gather.5.cloned.1.call-update
  18.0 0.7 all-gather.7.cloned.1.call-update
  18.7 0.6 reshape.418
  19.4 1.1 copy.62
  20.5 0.7 reduce_max.22
  21.7 23.9 %all-gather.9.cloned.1.call-done = bf16[2048,576]{1,0:T(8,128)(2,1)} async-done(((bf16[512,576]{1,0:T(8,128)(2,1)}), bf16[2048,576]{1,0:T(8,128)(2,1)}) %all-gather.9.cloned.1.call-update) | async-done | bytes 2359312 | tf_op jit(solution)/shard_map/all_gather | solution.py:83
  45.6 4.3 %copy.57 = bf16[1,4,512,576]{2,3,1,0:T(8,128)(2,1)} copy(bf16[1,4,512,576]{3,2,1,0:T(8,128)(2,1)} %bitcast.104) | data formatting | bytes 4718592
  49.9 70.6 %all-gather.5.cloned.1.call-done = bf16[512,4096]{1,0:T(8,128)(2,1)} async-done(((bf16[64,4096]{1,0:T(8,128)(2,1)}), bf16[512,4096]{1,0:T(8,128)(2,1)}) %all-gather.5.cloned.1.call-update) | async-done | bytes 4194320 | tf_op jit(solution)/shard_map/all_gather | solution.py:44
  120.6 6.5 %copy.53 = bf16[512,4096]{0,1:T(8,128)(2,1)} copy(bf16[512,4096]{1,0:T(8,128)(2,1)} %all-gather.5.cloned.1.call-done) | data formatting | bytes 8388608 | tf_op jit(solution)/shard_map/all_gather | solution.py:44
  127.1 2.2 fusion.20
  129.3 1.3 maximum_bitcast_fusion
  130.9 20.7 %while.20 = (s32[]{:T(128)}, f32[1,64,16]{1,2,0:T(8,128)S(1)}, f32[1,64,16]{1,2,0:T(8,128)S(1)}, f32[1,64,16,512]{3,2,1,0:T(8,128)S(1)}, s32[1,4]{1,0:T(1,128)S(...) while((s32[]{:T(128)}, f32[1,64,16]{1,2,0:T(8,128)S(1)}, ...), condition=%wide.region_8.9_spmd.clone, body=%wide.region_3.8_spmd.clone.sunk | while | flops 1146129920 | bytes 17670692 | solution.py:92
  130.9 0.6 fusion.55
  133.8 9.0 %conditional.3 = ((f32[1,64,16]{1,2,0:T(8,128)S(1)}, f32[1,64,16]{1,2,0:T(8,128)S(1)}, f32[1,64,16,512]{3,2,1,0:T(8,128)S(1)})) conditional(s32[]{:T(128)} %bitcast.97, (f32[1,64,16]{1,2,0:T(8,128)S(1)}, f32[1,64,16]{1,2,0:T(8,128)S(1)}, f32[1,64,16,512]{3,2,1,0:T(8,128)S(1)}) %tuple.70, (s32[1,512]{1,0:T(1,128)S(1)}, s32[1,1,64]{2,1,0:T(1,128)S(1)}, ...), branch_computations={%region_4.0_spmd, %region_5.7_spmd} | conditional | flops 1146129408 | bytes 17668416 | solution.py:90
  133.8 1.1 constant_dynamic-slice_fusion
  135.1 2.5 fusion.2
  137.6 0.7 fusion.5
  138.4 2.1 copy.47
  140.5 2.2 bitcast_add_fusion
  145.8 0.6 fusion.55
  152.0 2.4 fusion.26
  154.6 91.2 %all-gather.7.cloned.1.call-done = bf16[2048,2048]{1,0:T(8,128)(2,1)} async-done(((bf16[256,2048]{1,0:T(8,128)(2,1)}), bf16[2048,2048]{1,0:T(8,128)(2,1)}) %all-gather.7.cloned.1.call-update) | async-done | bytes 8388624 | tf_op jit(solution)/shard_map/all_gather | solution.py:98
  245.7 5.7 %fusion.12 = bf16[1,1,64,2048]{3,2,1,0:T(8,128)(2,1)} fusion(bf16[2048,2048]{1,0:T(8,128)(2,1)} %all-gather.7.cloned.1.call-done, bf16[8,8,16,128]{3,2,1,0:T(8,128)(2,1)S(1)} %bitcast.105), kind=kOutput, calls=%fused_computation.24 | convolution fusion | flops 537001984 | bytes 8912896 | tf_op jit(solution)/shard_map/dot_general | solution.py:99
  (54 shorter events, 7.6 us)
Async XLA Ops:
  7.2 38.5 %all-gather.9.cloned.1.call-start = ((), (), s32[]{:S(2)}) async-start(), calls=%async_computation.2 | async-start | bytes 3276800 | tf_op jit(solution)/shard_map/all_gather | solution.py:83
  12.0 6.7 %copy-start.4 = (bf16[1,1,64,3072]{3,2,1,0:T(8,128)(2,1)S(1)}, bf16[1,1,64,3072]{3,2,1,0:T(8,128)(2,1)}, u32[]{:S(2)}) copy-start(bf16[1,1,64,3072]{3,2,1,0:T(8,128)(2,1)} %param.12) | copy-start | bytes 1179652
  16.3 0.8 copy-start.1
  17.2 2.2 copy-start.2
  17.2 103.4 %all-gather.5.cloned.1.call-start = ((), (), s32[]{:S(2)}) async-start(), calls=%async_computation | async-start | bytes 4718592 | tf_op jit(solution)/shard_map/all_gather | solution.py:44
  18.0 227.8 %all-gather.7.cloned.1.call-start = ((), (), s32[]{:S(2)}) async-start(), calls=%async_computation.1 | async-start | bytes 9437184 | tf_op jit(solution)/shard_map/all_gather | solution.py:98
  19.3 2.4 copy-start.3
  49.9 77.1 %slice-start = ((bf16[1,1,64,16,192]{4,3,2,1,0:T(8,128)(2,1)}), bf16[1,1,64,16,128]{4,3,2,1,0:T(8,128)(2,1)S(1)}, s32[]{:S(2)}) async-start(bf16[1,1,64,16,192]{4,3,2,1,0:T(8,128)(2,1)} %copy-done.3), calls=%async_computation.3 | async-start | bytes 524288 | tf_op jit(solution)/shard_map/slice | solution.py:47
  129.3 1.6 copy-start.5
  135.0 2.6 %copy-start = (bf16[1,1,512,576]{2,3,1,0:T(8,128)(2,1)}, bf16[1,1,512,576]{2,3,1,0:T(8,128)(2,1)S(1)}, u32[]{:S(2)}) copy-start(bf16[1,1,512,576]{2,3,1,0:T(8,128)(2,1)S(1)} %constant_dynamic-slice_fusion) | copy-start | bytes 1769476 | tf_op jit(solution)/shard_map/while/body/eval_jaxpr/cond
Sparse Core Ops, SparseCore 0:
  17.3 28.2 all-gather.8
  47.7 72.7 all-gather.4
  122.7 122.9 all-gather.6
where the time goes:
time: 259 us; the launch traced here: 258 us
  waiting for transfers between devices  187 us (72%)
  local copies, waits for them, and re-layouts  21.7 us (8%)
  matrix products  15 us (6%)
  other arithmetic  14.7 us (6%)
  between operations  14 us (5%)
  loops' own time  5.23 us (2%)
    all_gather x1, waiting for transfers between devices, shards(): whole_out = lax.all_gather(out_weight, 'prompt', axis=0, tiled=True)  91.2 us
    all_gather x1, waiting for transfers between devices, shards(): lax.all_gather(kv_up, 'prompt', axis=0, tiled=True).reshape(LAT, H, DN + DV)  70.6 us
    all_gather x1, waiting for transfers between devices, shards(): piece = lax.all_gather(blended, 'group', axis=1, tiled=True)  23.9 us
    unnamed x14, local copies, waits for them, and re-layouts  7.73 us
    all_gather x1, local copies, waits for them, and re-layouts, shards(): lax.all_gather(kv_up, 'prompt', axis=0, tiled=True).reshape(LAT, H, DN + DV)  6.48 us
    dot_general x1, matrix products, shards(): attended = jnp.dot(heads, whole_out, preferred_element_type=jnp.float32)  5.65 us
  transfers between devices with their start and end apart: 3, of which 3 were waited for; matrix products, arithmetic and copies ran while one was open for 14% of the time, Pallas kernels for 0%

commit v1 on v0

--- a/solution.py
+++ b/solution.py
@@ -80,7 +80,14 @@
         jnp.zeros((prompts, rows, H), jnp.float32),
         jnp.zeros((prompts, rows, H, LAT), jnp.float32),
     )
-    piece = lax.all_gather(blended, "group", axis=1, tiled=True)
+    ring = [blended]
+    for hop in range(3):
+        ring.append(lax.ppermute(ring[-1], "group", [(dev, (dev + 1) % 4) for dev in range(4)]))
+    piece = jnp.roll(
+        jnp.concatenate(ring[::-1], axis=1),
+        (lax.axis_index("group") + 1) * ring[0].shape[1],
+        axis=1,
+    )
 
     def one_group(index, carry):
         keys = lax.dynamic_slice_in_dim(piece, index, 1, 1)[:, 0]

time: 259 us -> 225 us (0.87)
  waiting for transfers between devices: 187 us -> 154 us
    all_gather x1, waiting for transfers between devices: 70.6 us -> 36.3 us  [shards(): lax.all_gather(kv_up, 'prompt', axis=0, tiled=True).reshape(LAT, H, DN + DV)]
    ppermute x0 -> x3, waiting for transfers between devices: none -> 25.1 us  [shards(): lax.ppermute(ring[-1], 'group', [(dev, (dev + 1) % 4) for dev in range(4)])]
    all_gather x1 -> x0, waiting for transfers between devices: 23.9 us -> none  [shards(): piece = lax.all_gather(blended, 'group', axis=1, tiled=True)]
    unnamed x14 -> x24, local copies, waits for them, and re-layouts: 7.73 us -> 4.67 us
  transfers between devices with their start and end apart: 3 -> 5, of which waited for: 3 -> 5; matrix products, arithmetic and copies ran while one was open for 14% -> 20% of each run, Pallas kernels for 0% -> 0%
where the time goes in v1:
time: 225 us; the launch traced here: 223 us
  waiting for transfers between devices  154 us (68%)
  local copies, waits for them, and re-layouts  21.2 us (9%)
  matrix products  15.1 us (7%)
  between operations  14.4 us (6%)
  other arithmetic  13.3 us (6%)
  loops' own time  5.04 us (2%)
    all_gather x1, waiting for transfers between devices, shards(): whole_out = lax.all_gather(out_weight, 'prompt', axis=0, tiled=True)  91 us
    all_gather x1, waiting for transfers between devices, shards(): lax.all_gather(kv_up, 'prompt', axis=0, tiled=True).reshape(LAT, H, DN + DV)  36.3 us
    ppermute x3, waiting for transfers between devices, shards(): lax.ppermute(ring[-1], 'group', [(dev, (dev + 1) % 4) for dev in range(4)])  25.1 us
    all_gather x1, local copies, waits for them, and re-layouts, shards(): lax.all_gather(kv_up, 'prompt', axis=0, tiled=True).reshape(LAT, H, DN + DV)  6.47 us
    dot_general x1, matrix products, shards(): attended = jnp.dot(heads, whole_out, preferred_element_type=jnp.float32)  5.65 us
    another operation x1, loops' own time, shards(): lax.fori_loop(0, piece.shape[1], one_group, start_state)  4.92 us
    unnamed x24, local copies, waits for them, and re-layouts  4.67 us
  transfers between devices with their start and end apart: 5, of which 5 were waited for; matrix products, arithmetic and copies ran while one was open for 20% of the time, Pallas kernels for 0%

profile of v1, /device:TPU:0, one launch (start us, length us, event | category | flops | bytes accessed | tf_op | source)
XLA Modules:
  0.0 223.3 jit_solution(17424806439999960745)
XLA Ops:
  7.2 0.7 all-gather.3.cloned.1.call-update
  8.0 0.7 all-gather.5.cloned.1.call-update
  8.7 0.7 slice.44
  9.5 1.2 fusion.52
  10.8 1.3 convert_bitcast_fusion
  12.5 1.4 copy.55
  14.1 1.3 scatter_custom_fusion
  16.2 9.5 %collective-permute-done = bf16[1,1,512,576]{2,3,1,0:T(8,128)(2,1)S(1)} collective-permute-done((bf16[1,1,512,576]{2,3,1,0:T(8,128)(2,1)S(1)}, bf16[1,1,512,576]{2,3,1,0:T(8,128)(2,1)S(1)}, u32[]{:S(2)}, u32[]{:S(2)}) %collective-permute-start) | collective-permute-done | bytes 589856 | tf_op jit(solution)/shard_map/ppermute | solution.py:85
  25.7 9.3 %collective-permute-done.1 = bf16[1,1,512,576]{2,3,1,0:T(8,128)(2,1)S(1)} collective-permute-done((bf16[1,1,512,576]{2,3,1,0:T(8,128)(2,1)S(1)}, bf16[1,1,512,576]{2,3,1,0:T(8,128)(2,1)S(1)}, u32[]{:S(2)}, u32[]{:S(2)}) %collective-permute-start.1) | collective-permute-done | bytes 589856 | tf_op jit(solution)/shard_map/ppermute | solution.py:85
  35.9 0.6 reduce_max.22
  36.6 0.9 subtract_convert_fusion
  38.1 6.3 %collective-permute-done.2 = bf16[1,1,512,576]{2,3,1,0:T(8,128)(2,1)} collective-permute-done((bf16[1,1,512,576]{2,3,1,0:T(8,128)(2,1)S(1)}, bf16[1,1,512,576]{2,3,1,0:T(8,128)(2,1)}, u32[]{:S(2)}, u32[]{:S(2)}) %collective-permute-start.2) | collective-permute-done | bytes 589856 | tf_op jit(solution)/shard_map/ppermute | solution.py:85
  44.4 1.4 copy.60
  46.8 2.5 %copy.70 = bf16[1,4,512,576]{2,3,1,0:T(8,128)(2,1)} copy(bf16[1,4,512,576]{3,2,1,0:T(8,128)(2,1)S(1)} %constant_dynamic-slice_fusion.2) | data formatting | bytes 4718592
  49.4 36.3 %all-gather.3.cloned.1.call-done = bf16[512,4096]{1,0:T(8,128)(2,1)} async-done(((bf16[64,4096]{1,0:T(8,128)(2,1)}), bf16[512,4096]{1,0:T(8,128)(2,1)}) %all-gather.3.cloned.1.call-update) | async-done | bytes 4194320 | tf_op jit(solution)/shard_map/all_gather | solution.py:44
  85.7 6.5 %copy.66 = bf16[512,4096]{0,1:T(8,128)(2,1)} copy(bf16[512,4096]{1,0:T(8,128)(2,1)} %all-gather.3.cloned.1.call-done) | data formatting | bytes 8388608 | tf_op jit(solution)/shard_map/all_gather | solution.py:44
  92.1 2.2 %fusion.20 = bf16[1,1,64,16,512]{4,2,3,1,0:T(8,128)(2,1)S(1)} fusion(bf16[512,16,256]{0,2,1:T(8,128)(2,1)} %bitcast.102, bf16[1,1,64,16,128]{4,3,2,1,0:T(8,128)(2,1)S(1)} %slice-done), kind=kOutput, calls=%fused_computation.31 | convolution fusion | flops 134742016 | bytes 3407872 | tf_op jit(solution)/shard_map/pcshd,lhd->pcshl/dot_general | solution.py:46
  94.4 1.3 maximum_bitcast_fusion
  96.0 20.9 %while.20 = (s32[]{:T(128)}, f32[1,64,16]{1,2,0:T(8,128)S(1)}, f32[1,64,16]{1,2,0:T(8,128)S(1)}, f32[1,64,16,512]{3,2,1,0:T(8,128)S(1)}, s32[1,4]{1,0:T(1,128)S(...) while((s32[]{:T(128)}, f32[1,64,16]{1,2,0:T(8,128)S(1)}, ...), condition=%wide.region_8.9_spmd.clone, body=%wide.region_3.8_spmd.clone.sunk | while | flops 1146129920 | bytes 17670692 | solution.py:99
  96.6 0.6 iota_add_fusion.2
  99.0 9.0 %conditional.3 = ((f32[1,64,16]{1,2,0:T(8,128)S(1)}, f32[1,64,16]{1,2,0:T(8,128)S(1)}, f32[1,64,16,512]{3,2,1,0:T(8,128)S(1)})) conditional(s32[]{:T(128)} %bitcast.98, (f32[1,64,16]{1,2,0:T(8,128)S(1)}, f32[1,64,16]{1,2,0:T(8,128)S(1)}, f32[1,64,16,512]{3,2,1,0:T(8,128)S(1)}) %tuple.69, (s32[1,512]{1,0:T(1,128)S(1)}, s32[1,1,64]{2,1,0:T(1,128)S(1)}, ...), branch_computations={%region_4.4_spmd, %region_5.7_spmd} | conditional | flops 1146129408 | bytes 17668416 | solution.py:97
  99.0 1.1 constant_dynamic-slice_fusion
  100.2 2.5 %fusion.2 = (f32[64,16]{0,1:T(8,128)S(1)}, f32[512,64,16]{0,1,2:T(8,128)S(1)}) fusion(pred[64,512]{1,0:T(8,128)(4,1)S(1)} %broadcast_compare_fusion, bf16[1,64,16,576]{3,1,2,0:T(8,128)(2,1)} %get-tuple-element.279, bf16[1,1,512,576]{2,3,1,0:T(8,128)(2,1)S(1)} %constant_dynamic-slice_fusion), kind=kOutput, calls=%fused_computation.5 | convolution fusion | flops 605551616 | bytes 3903488 | tf_op jit(solution)/shard_map/while/body/eval_jaxpr/cond/branch_1_fun/pqhe,pke->pqhk/dot_general | solution.py:62
  102.8 0.7 fusion.5
  103.6 2.1 copy.53
  105.7 2.2 %bitcast_add_fusion = f32[1,64,16,512]{3,2,1,0:T(8,128)S(1)} fusion(f32[1,64,16,512]{3,2,1,0:T(8,128)S(1)} %get-tuple-element.281, bf16[64,16,512]{2,0,1:T(8,128)(2,1)S(1)} %get-tuple-element.380, f32[64,16]{1,0:T(8,128)S(1)} %copy.52, bf16[1,512,576]{2,1,0:T(8,128)(2,1)} %bitcast.99), kind=kOutput, calls=%fused_computation.2 | convolution fusion | flops 537919488 | bytes 5771264 | tf_op jit(solution)/shard_map/while/body/eval_jaxpr/cond/branch_1_fun/pqhk,pkl->pqhl/dot_general | solution.py:70
  108.6 0.6 iota_add_fusion.2
  111.6 0.6 iota_add_fusion.2
  114.6 0.6 iota_add_fusion.2
  117.3 2.4 %fusion.26 = bf16[1,64,16,128]{3,1,2,0:T(8,128)(2,1)S(1)} fusion(bf16[512,16,256]{0,2,1:T(8,128)(2,1)} %bitcast.103, bf16[64,16,512]{2,1,0:T(8,128)(2,1)S(1)} %fusion.30), kind=kOutput, calls=%fused_computation.34 | convolution fusion | flops 134348800 | bytes 3407872 | tf_op jit(solution)/shard_map/pqhl,lhv->pqhv/dot_general | solution.py:101
  119.9 91.0 %all-gather.5.cloned.1.call-done = bf16[2048,2048]{1,0:T(8,128)(2,1)} async-done(((bf16[256,2048]{1,0:T(8,128)(2,1)}), bf16[2048,2048]{1,0:T(8,128)(2,1)}) %all-gather.5.cloned.1.call-update) | async-done | bytes 8388624 | tf_op jit(solution)/shard_map/all_gather | solution.py:105
  210.9 5.7 %fusion.12 = bf16[1,1,64,2048]{3,2,1,0:T(8,128)(2,1)} fusion(bf16[2048,2048]{1,0:T(8,128)(2,1)} %all-gather.5.cloned.1.call-done, bf16[8,8,16,128]{3,2,1,0:T(8,128)(2,1)S(1)} %bitcast.105), kind=kOutput, calls=%fused_computation.24 | convolution fusion | flops 537001984 | bytes 8912896 | tf_op jit(solution)/shard_map/dot_general | solution.py:106
  (73 shorter events, 9.4 us)
Async XLA Ops:
  7.2 6.7 %copy-start.5 = (bf16[1,1,64,576]{3,2,1,0:T(8,128)(2,1)S(1)}, bf16[1,1,64,576]{3,2,1,0:T(8,128)(2,1)}, u32[]{:S(2)}) copy-start(bf16[1,1,64,576]{3,2,1,0:T(8,128)(2,1)} %param.13) | copy-start | bytes 221188
  7.2 6.7 %copy-start.6 = (bf16[512]{0:T(512)(128)(2,1)S(1)}, bf16[512]{0:T(512)(128)(2,1)}, u32[]{:S(2)}) copy-start(bf16[512]{0:T(512)(128)(2,1)} %param.17) | copy-start | bytes 3076
  7.2 78.5 %all-gather.3.cloned.1.call-start = ((), (), s32[]{:S(2)}) async-start(), calls=%async_computation | async-start | bytes 4718592 | tf_op jit(solution)/shard_map/all_gather | solution.py:44
  7.9 27.3 %copy-start.4 = (bf16[1,1,64,3072]{3,2,1,0:T(8,128)(2,1)S(1)}, bf16[1,1,64,3072]{3,2,1,0:T(8,128)(2,1)}, u32[]{:S(2)}) copy-start(bf16[1,1,64,3072]{3,2,1,0:T(8,128)(2,1)} %param.12) | copy-start | bytes 1179652
  7.9 202.9 %all-gather.5.cloned.1.call-start = ((), (), s32[]{:S(2)}) async-start(), calls=%async_computation.1 | async-start | bytes 9437184 | tf_op jit(solution)/shard_map/all_gather | solution.py:105
  15.7 19.6 %copy-start.3 = (bf16[1,1,512,576]{2,3,1,0:T(8,128)(2,1)}, bf16[1,1,512,576]{2,3,1,0:T(8,128)(2,1)S(1)}, u32[]{:S(2)}) copy-start(bf16[1,1,512,576]{2,3,1,0:T(8,128)(2,1)S(1)} %copy.59) | copy-start | bytes 1769476
  15.7 10.0 %collective-permute-start = (bf16[1,1,512,576]{2,3,1,0:T(8,128)(2,1)S(1)}, bf16[1,1,512,576]{2,3,1,0:T(8,128)(2,1)S(1)}, u32[]{:S(2)}, u32[]{:S(2)}) collective-permute-start(bf16[1,1,512,576]{2,3,1,0:T(8,128)(2,1)S(1)} %copy.59), channel_id=1, source_target_pairs={{0,8},{8,16},{16,24},{24,0},{1,9},{9,17},{17,25},{25,1},{2,10},{10... | collective-permute-start | bytes 1769480 | tf_op jit(solution)/shard_map/ppermute | solution.py:85
  25.7 9.3 %collective-permute-start.1 = (bf16[1,1,512,576]{2,3,1,0:T(8,128)(2,1)S(1)}, bf16[1,1,512,576]{2,3,1,0:T(8,128)(2,1)S(1)}, u32[]{:S(2)}, u32[]{:S(2)}) collective-permute-start(bf16[1,1,512,576]{2,3,1,0:T(8,128)(2,1)S(1)} %collective-permute-done), channel_id=1, source_target_pairs={{0,8},{8,16},{16,24},{24,0},{1,9},{9,17},{17,25},{25,1},{2,10},{10... | collective-permute-start | bytes 1769480 | tf_op jit(solution)/shard_map/ppermute | solution.py:85
  35.0 9.4 %collective-permute-start.2 = (bf16[1,1,512,576]{2,3,1,0:T(8,128)(2,1)S(1)}, bf16[1,1,512,576]{2,3,1,0:T(8,128)(2,1)}, u32[]{:S(2)}, u32[]{:S(2)}) collective-permute-start(bf16[1,1,512,576]{2,3,1,0:T(8,128)(2,1)S(1)} %collective-permute-done.1), channel_id=1, source_target_pairs={{0,8},{8,16},{16,24},{24,0},{1,9},{9,17},{17,25},{25,1},{2,10},{10... | collective-permute-start | bytes 1769480 | tf_op jit(solution)/shard_map/ppermute | solution.py:85
  35.9 2.0 copy-start.1
  49.4 42.8 %slice-start = ((bf16[1,1,64,16,192]{4,3,2,1,0:T(8,128)(2,1)}), bf16[1,1,64,16,128]{4,3,2,1,0:T(8,128)(2,1)S(1)}, s32[]{:S(2)}) async-start(bf16[1,1,64,16,192]{4,3,2,1,0:T(8,128)(2,1)} %copy-done.1), calls=%async_computation.2 | async-start | bytes 524288 | tf_op jit(solution)/shard_map/slice | solution.py:47
  92.1 2.3 %copy-start.2 = (bf16[1,1,64,16,32]{4,2,3,1,0:T(8,128)(2,1)S(1)}, bf16[1,1,64,16,32]{4,2,3,1,0:T(8,128)(2,1)}, u32[]{:S(2)}) copy-start(bf16[1,1,64,16,32]{4,2,3,1,0:T(8,128)(2,1)} %get-tuple-element.385) | copy-start | bytes 196612
  94.4 1.6 copy-start.7
  100.1 2.6 %copy-start = (bf16[1,1,512,576]{2,3,1,0:T(8,128)(2,1)}, bf16[1,1,512,576]{2,3,1,0:T(8,128)(2,1)S(1)}, u32[]{:S(2)}) copy-start(bf16[1,1,512,576]{2,3,1,0:T(8,128)(2,1)S(1)} %constant_dynamic-slice_fusion) | copy-start | bytes 1769476 | tf_op jit(solution)/shard_map/while/body/eval_jaxpr/cond
Sparse Core Ops, SparseCore 0:
  10.1 75.5 all-gather.2
  87.8 123.0 all-gather.4
